TPU v7x, 128 devices: a whole 4x4x4 slice. The times are simulated.
128 devices in a mesh: dom: 4 (over y_hi, core), dim: 32 (over z, y_lo, x).
Axes of the slice: x: 4, y: 4 (y_hi: 2, y_lo: 2; y = y_hi * 2 + y_lo), z: 4, core: 2. Of those that a mesh axis runs over, the one named last changes fastest.
Arguments:
- particles: float32 [512, 262144], P('dom', 'dim'), may hold values from -16 to 16
- scores: float32 [512, 262144], P('dom', 'dim'), may hold values from -0.00036621094 to 0.00036621094
- spread: float32 [], replicated, may hold values from 131072 to 262144
- step_size: float32 [], replicated, may hold values from 4194304 to 8388608
Outputs:
- new_particles: float32 [512, 262144], P('dom', 'dim')
All inputs are finite; a program needn't handle non-finite values.
Results may differ from a plain program's by a relative error of at most 0.000064.
Values sent between devices are 32-bit elements; how exact they have to be, the bound alone decides.
A program may use at most 128 MiB of HBM per device.

v0:
```python
import jax
import jax.numpy as jnp
from jax import lax
from jax.sharding import PartitionSpec as P


def cut_along(array, dim, devices):
    dims = array.shape
    blocks = array.reshape(*dims[:dim], devices, dims[dim] // devices, *dims[dim + 1 :])
    return jnp.moveaxis(blocks, dim, 0)


def sum_at_owner(array, axis, dim):
    blocks = cut_along(array, dim, lax.axis_size(axis))
    arrived = lax.all_to_all(blocks, axis, split_axis=0, concat_axis=0, tiled=True)
    return arrived.sum(axis=0)


def from_everyone(array, axis):
    devices = lax.axis_size(axis)
    return lax.all_to_all(
        jnp.broadcast_to(array[None], (devices, *array.shape)), axis, 0, 0, tiled=True
    )


def over_copies(array, axis):
    everything = from_everyone(array, axis)
    return jnp.sum(everything, axis=0)


def in_order(blocks, dim):
    dims = list(blocks.shape[1:])
    dims[dim] *= blocks.shape[0]
    return jnp.moveaxis(blocks, 0, dim).reshape(dims)


def gathered_copies(array, axis, dim):
    return in_order(from_everyone(array, axis), dim)


def on_device(particles, scores, spread, step_size):
    precise = lax.Precision.HIGHEST
    local_rows = particles.shape[0]
    count_all = local_rows * lax.axis_size("dom")
    gathered = lax.all_gather(particles, "dom", axis=0, tiled=True)
    product = lax.dot_general(
        particles,
        gathered,
        (((1,), (1,)), ((), ())),
        precision=precise,
        preferred_element_type=jnp.float32,
    )
    norms = jnp.sum(gathered * gathered, axis=1)
    gram_share, square_share = (sum_at_owner(product, "dim", 1), sum_at_owner(norms, "dim", 0))
    own_squares = over_copies(jnp.sum(particles * particles, axis=1), "dim")
    kernel_share = jnp.exp(
        -(own_squares[:, None] + square_share[None, :] - 2.0 * gram_share) / spread
    )
    kernel = gathered_copies(kernel_share, "dim", 1)
    attract = jnp.dot(
        kernel,
        lax.all_gather(scores, "dom", axis=0, tiled=True),
        precision=precise,
        preferred_element_type=jnp.float32,
    )
    pulled = jnp.dot(kernel, gathered, precision=precise, preferred_element_type=jnp.float32)
    weight_sum = jnp.sum(kernel, axis=1, keepdims=True)
    update = (attract + 2.0 / spread * (weight_sum * particles - pulled)) / count_all
    return particles + step_size * update


def solution(mesh):
    return jax.shard_map(
        on_device,
        mesh=mesh,
        in_specs=(P("dom", "dim"), P("dom", "dim"), P(), P()),
        out_specs=P("dom", "dim"),
        check_vma=False,
    )
```

profile of v0, /device:TPU:1, one launch (start us, length us, event | category | flops | bytes accessed | tf_op | source)
XLA Modules:
  0.0 261.2 jit_solution(14739660811756581120)
XLA Ops:
  6.5 0.0 all-gather.3.cloned.1.call-start
  6.5 0.7 all-gather.3.cloned.1.call-update
  7.3 0.0 all-gather.5.cloned.1.call-start
  7.3 0.7 all-gather.5.cloned.1.call-update
  8.0 2.5 multiply_reduce_fusion.1
  10.5 0.6 broadcast_in_dim.4
  11.2 9.7 %all-to-all-start = ((f32[32,1,128]{2,1,0:T(1,128)}), f32[32,1,128]{2,1,0:T(1,128)S(1)}, u32[]{:S(2)}, u32[]{:S(2)}) async-start(f32[32,1,128]{2,1,0:T(1,128)} %broadcast_in_dim.4), calls=%async_computation | async-start | bytes 32768 | tf_op jit(solution)/shard_map/all_to_all | solution.py:21
  20.9 101.7 %all-gather.3.cloned.1.call-done = f32[512,8192]{1,0:T(8,128)} async-done(((f32[128,8192]{1,0:T(8,128)}), f32[512,8192]{1,0:T(8,128)}) %all-gather.3.cloned.1.call-update) | async-done | bytes 16777232 | tf_op jit(solution)/shard_map/all_gather | solution.py:45
  122.6 7.0 %multiply_reduce_fusion = f32[512]{0:T(512)S(1)} fusion(f32[512,8192]{1,0:T(8,128)} %all-gather.3.cloned.1.call-done), kind=kLoop, calls=%fused_computation | loop fusion | flops 8388096 | bytes 16779264 | tf_op jit(solution)/shard_map/reduce_sum | solution.py:53
  129.6 0.7 all_to_all.17
  130.2 0.0 all-to-all-done
  130.2 7.0 %all-to-all-start.1 = ((f32[32,1,16]{2,1,0:T(1,128)}), f32[32,1,16]{2,1,0:T(1,128)S(1)}, u32[]{:S(2)}, u32[]{:S(2)}) async-start(f32[32,1,16]{2,1,0:T(1,128)} %bitcast.1), calls=%async_computation.1 | async-start | bytes 32768 | tf_op jit(solution)/shard_map/all_to_all | solution.py:15
  137.2 17.7 %fusion.3 = f32[128,512]{0,1:T(8,128)} fusion(f32[128,8192]{1,0:T(8,128)} %param.4, f32[512,8192]{1,0:T(8,128)} %all-gather.3.cloned.1.call-done), kind=kOutput, calls=%fused_computation.8 | convolution fusion | flops 6442450944 | bytes 21233664 | tf_op jit(solution)/shard_map/dot_general | solution.py:46
  155.0 0.0 all-to-all-done.1
  155.0 7.8 %all-to-all-start.2 = ((f32[32,128,16]{1,2,0:T(8,128)}), f32[32,128,16]{1,2,0:T(8,128)S(1)}, u32[]{:S(2)}, u32[]{:S(2)}) async-start(f32[32,128,16]{1,2,0:T(8,128)} %bitcast.3), calls=%async_computation.2 | async-start | bytes 524288 | tf_op jit(solution)/shard_map/all_to_all | solution.py:15
  163.4 0.1 reduce_sum.57
  163.5 7.5 %all-to-all-done.2 = f32[32,128,16]{1,2,0:T(8,128)S(1)} async-done(((f32[32,128,16]{1,2,0:T(8,128)}), f32[32,128,16]{1,2,0:T(8,128)S(1)}, u32[]{:S(2)}, u32[]{:S(2)}) %all-to-all-start.2) | async-done | bytes 262176 | tf_op jit(solution)/shard_map/all_to_all | solution.py:15
  171.0 0.1 divide_exponential_fusion
  171.1 0.7 broadcast_in_dim.5
  171.8 5.5 %all-to-all-start.3 = ((f32[32,128,16]{1,2,0:T(8,128)}), f32[32,128,16]{1,2,0:T(8,128)S(1)}, u32[]{:S(2)}, u32[]{:S(2)}) async-start(f32[32,128,16]{1,2,0:T(8,128)} %broadcast_in_dim.5), calls=%async_computation.3 | async-start | bytes 524288 | tf_op jit(solution)/shard_map/all_to_all | solution.py:21
  178.0 7.3 %all-to-all-done.3 = f32[32,128,16]{1,2,0:T(8,128)S(1)} async-done(((f32[32,128,16]{1,2,0:T(8,128)}), f32[32,128,16]{1,2,0:T(8,128)S(1)}, u32[]{:S(2)}, u32[]{:S(2)}) %all-to-all-start.3) | async-done | bytes 262176 | tf_op jit(solution)/shard_map/all_to_all | solution.py:21
  185.4 0.1 reduce_sum.59
  185.4 14.4 %fusion = f32[128,8192]{1,0:T(8,128)} fusion(f32[128,512]{0,1:T(8,128)S(1)} %bitcast.14, f32[512,8192]{1,0:T(8,128)} %all-gather.3.cloned.1.call-done, f32[128,8192]{1,0:T(8,128)} %param.4, f32[128]{0:T(128)S(1)} %reduce_sum.59, f32[]{:T(128)S(6)} %div.17), kind=kOutput, calls=%fused_computation.2 | convolution fusion | flops 6445596672 | bytes 25428484 | tf_op jit(solution)/shard_map/dot_general | solution.py:66
  199.8 39.6 %all-gather.5.cloned.1.call-done = f32[512,8192]{1,0:T(8,128)} async-done(((f32[128,8192]{1,0:T(8,128)}), f32[512,8192]{1,0:T(8,128)}) %all-gather.5.cloned.1.call-update) | async-done | bytes 16777232 | tf_op jit(solution)/shard_map/all_gather | solution.py:62
  239.4 15.0 %fusion.2 = f32[128,8192]{1,0:T(8,128)} fusion(f32[128,8192]{1,0:T(8,128)} %param.4, f32[128,8192]{1,0:T(8,128)} %fusion, f32[128,512]{0,1:T(8,128)S(1)} %bitcast.15, f32[512,8192]{1,0:T(8,128)} %all-gather.5.cloned.1.call-done, f32[]{:T(128)S(6)} %mul.46), kind=kOutput, calls=%fused_computation.5 | convolution fusion | flops 6445596672 | bytes 29622276 | tf_op jit(solution)/shard_map/dot_general | solution.py:60
  (2 shorter events, 0.1 us)
Async XLA Ops:
  6.5 116.1 %all-gather.3.cloned.1.call-start = ((), (), s32[]{:S(2)}) async-start(), calls=%async_computation.4 | async-start | bytes 20971520 | tf_op jit(solution)/shard_map/all_gather | solution.py:45
  7.3 232.1 %all-gather.5.cloned.1.call-start = ((), (), s32[]{:S(2)}) async-start(), calls=%async_computation.5 | async-start | bytes 20971520 | tf_op jit(solution)/shard_map/all_gather | solution.py:62
  11.2 119.1 %all-to-all-start = ((f32[32,1,128]{2,1,0:T(1,128)}), f32[32,1,128]{2,1,0:T(1,128)S(1)}, u32[]{:S(2)}, u32[]{:S(2)}) async-start(f32[32,1,128]{2,1,0:T(1,128)} %broadcast_in_dim.4), calls=%async_computation | async-start | bytes 32768 | tf_op jit(solution)/shard_map/all_to_all | solution.py:21
  130.2 24.7 %all-to-all-start.1 = ((f32[32,1,16]{2,1,0:T(1,128)}), f32[32,1,16]{2,1,0:T(1,128)S(1)}, u32[]{:S(2)}, u32[]{:S(2)}) async-start(f32[32,1,16]{2,1,0:T(1,128)} %bitcast.1), calls=%async_computation.1 | async-start | bytes 32768 | tf_op jit(solution)/shard_map/all_to_all | solution.py:15
  155.0 16.0 %all-to-all-start.2 = ((f32[32,128,16]{1,2,0:T(8,128)}), f32[32,128,16]{1,2,0:T(8,128)S(1)}, u32[]{:S(2)}, u32[]{:S(2)}) async-start(f32[32,128,16]{1,2,0:T(8,128)} %bitcast.3), calls=%async_computation.2 | async-start | bytes 524288 | tf_op jit(solution)/shard_map/all_to_all | solution.py:15
  171.8 13.5 %all-to-all-start.3 = ((f32[32,128,16]{1,2,0:T(8,128)}), f32[32,128,16]{1,2,0:T(8,128)S(1)}, u32[]{:S(2)}, u32[]{:S(2)}) async-start(f32[32,128,16]{1,2,0:T(8,128)} %broadcast_in_dim.5), calls=%async_computation.3 | async-start | bytes 524288 | tf_op jit(solution)/shard_map/all_to_all | solution.py:21
Sparse Core Ops, SparseCore 0:
  9.0 113.5 all-gather.2
  124.3 115.0 all-gather.4
where the time goes:
time: 262 us; the launch traced here: 261 us
  waiting for transfers between devices  157 us (60%)
  matrix products  47.1 us (18%)
  starting transfers between devices  30 us (11%)
  between operations  14.8 us (6%)
  other arithmetic  9.76 us (4%)
    all_gather x1, waiting for transfers between devices, on_device(): gathered = lax.all_gather(particles, 'dom', axis=0, tiled=True)  102 us
    all_gather x1, waiting for transfers between devices, on_device(): lax.all_gather(scores, 'dom', axis=0, tiled=True)  39.6 us
    dot_general x1, matrix products, on_device(): lax.dot_general(particles, gathered, (((1,), (1,)), ((), ())), precision=...  17.7 us
    all_to_all x2, starting transfers between devices, from_everyone(): lax.all_to_all(jnp.broadcast_to(array[None], (devices, *array.shape)), ax...  15.2 us
    dot_general x1, matrix products, on_device(): jnp.dot(kernel, lax.all_gather(scores, 'dom', axis=0, tiled=True), precis...  15 us
    all_to_all x2, starting transfers between devices, sum_at_owner(): lax.all_to_all(blocks, axis, split_axis=0, concat_axis=0, tiled=True)  14.8 us
    dot_general x1, matrix products, on_device(): jnp.dot(kernel, gathered, precision=precise, preferred_element_type=jnp.f...  14.4 us
    all_to_all x2, waiting for transfers between devices, sum_at_owner(): lax.all_to_all(blocks, axis, split_axis=0, concat_axis=0, tiled=True)  7.48 us
  transfers between devices with their start and end apart: 6, of which 4 were waited for; matrix products, arithmetic and copies ran while one was open for 17% of the time, Pallas kernels for 0%

commit v1 on v0

v1 whole, which is shorter than its diff:
```python
import functools

import jax
import jax.numpy as jnp
from jax import lax
from jax.experimental import pallas as pl
from jax.experimental.pallas import tpu as pltpu
from jax.sharding import PartitionSpec as P

MESH = pl.DeviceIdType.MESH
PARTS = 4
EARLY = 3


def body(
    size_dom, rows, quarter,
    scal, p_ref, s_ref, out_ref,
    pb, sb, pt, qs, ob, gram, half_in, xin, zin, yin, full, k_own, k_oth, w_ref,
    load_sem, sib_send, sib_recv, p_send, p_recv, s_send, s_recv, q_send, q_recv,
    red_send, red_recv, x_send, x_recv, z_send, z_recv, y_send, y_recv,
    gz_send, gz_recv, gx_send, gx_recv, gc_send, gc_recv,
    o_local, o_send, o_recv,
):
    piece = quarter // PARTS
    dom, dim = lax.axis_index("dom"), lax.axis_index("dim")
    h, c = dom // 2, lax.rem(dom, 2)
    z, lo, x = dim // 8, lax.rem(dim // 4, 2), lax.rem(dim, 4)
    y = h * 2 + lo
    block = dom

    def dev(hh, cc, zz, ll, xx):
        return (hh * 2 + cc, zz * 8 + ll * 4 + xx)

    sib = dev(h, 1 - c, z, lo, x)
    over = [dev(1 - h, cc, z, lo, x) for cc in range(2)]
    xs = [dev(h, c, z, lo, lax.rem(x + d, 4)) for d in (1, 2, 3)]
    zs = [dev(h, c, lax.rem(z + d, 4), lo, x) for d in (1, 2, 3)]
    ys = []
    for d in (1, 2, 3):
        yy = lax.rem(y + d, 4)
        ys.append(dev(yy // 2, c, z, lax.rem(yy, 2), x))
    cross = dev(1 - h, 1 - c, z, lo, x)

    barrier = pltpu.get_barrier_semaphore()
    peers = [sib, cross, *xs, *zs, *ys]
    for peer in peers:
        pl.semaphore_signal(barrier, inc=1, device_id=peer, device_id_type=MESH)
    pl.semaphore_wait(barrier, len(peers))

    def remote(src, dst, ssem, rsem, to):
        return pltpu.make_async_remote_copy(
            src_ref=src, dst_ref=dst, send_sem=ssem, recv_sem=rsem,
            device_id=to, device_id_type=MESH,
        )

    def cols(cc, g, k, width):
        return pl.ds(pl.multiple_of(cc * (2 * quarter) + g * quarter + k * piece, piece), width)

    def mine(b):
        return pl.ds(pl.multiple_of(b * rows, rows), rows)

    def kcols(k):
        return pl.ds(pl.multiple_of(k * piece, piece), piece)

    side = [h, 1 - h]

    def p_copy(cc, k):
        return remote(p_ref.at[:, cols(cc, 1 - h, k, piece)], pb.at[0, mine(block), kcols(k)],
                      p_send.at[cc, k], p_recv.at[c, k], over[cc])

    def s_copy(cc, k):
        return remote(s_ref.at[:, cols(cc, 1 - h, k, piece)], sb.at[0, mine(block), kcols(k)],
                      s_send.at[cc, k], s_recv.at[c, k], over[cc])

    def q_copy(cc, k):
        return remote(qs.at[cc, :, kcols(k)], sb.at[1, mine(block), kcols(k)],
                      q_send.at[cc, k], q_recv.at[c, k], over[cc])

    def arrival(buf, gi, cc, k, ssem, rsem):
        there = buf.at[gi, mine((1 - h) * 2 + cc), kcols(k)]
        return remote(there, there, ssem.at[cc, k], rsem.at[cc, k], over[cc])

    def sib_copy(n, gi):
        src, dst = ((p_ref, pb), (s_ref, sb))[n]
        return remote(src.at[:, cols(1 - c, side[gi], 0, quarter)], dst.at[gi, mine(block), :],
                      sib_send.at[n, gi], sib_recv.at[n, gi], sib)

    for k in range(PARTS):
        for cc in range(2):
            p_copy(cc, k).start()
    loads = []
    for n, (src, dst) in enumerate(((p_ref, pb), (s_ref, sb))):
        for gi in range(2):
            loads.append(pltpu.make_async_copy(
                src.at[:, cols(c, side[gi], 0, quarter)], dst.at[gi, mine(block), :], load_sem.at[2 * n + gi]))
    for cc in range(2):
        loads.append(pltpu.make_async_copy(p_ref.at[:, cols(cc, h, 0, quarter)], pt.at[cc], load_sem.at[4 + cc]))
        loads.append(pltpu.make_async_copy(s_ref.at[:, cols(cc, h, 0, quarter)], qs.at[cc], load_sem.at[6 + cc]))
    for n in range(2):
        for gi in range(2):
            sib_copy(n, gi).start()
    for load in loads:
        load.start()
    for k in range(EARLY):
        for cc in range(2):
            s_copy(cc, k).start()
    for load in loads:
        load.wait()

    spread = jnp.full((1, 128), scal[0], jnp.float32)
    pull = (2.0 / spread)[:, :1]
    for cc in range(2):
        def scale(k, carry, cc=cc):
            qs[cc, :, kcols(k)] = qs[cc, :, kcols(k)] - pull * pt[cc, :, kcols(k)]
            return carry
        lax.fori_loop(0, PARTS, scale, 0)

    sib_copy(0, 0).wait_recv()
    gram[...] = jnp.zeros_like(gram)

    def gram_step(k, carry):
        for cc in range(2):
            arrival(pb, 0, cc, k, p_send, p_recv).wait_recv()
        part = pb[0, :, kcols(k)]
        gram[...] += lax.dot_general(part, part, (((1,), (1,)), ((), ())),
                                     precision=lax.Precision.HIGHEST, preferred_element_type=jnp.float32)
        return carry

    lax.fori_loop(0, PARTS, gram_step, 0)

    count = size_dom * rows
    n_c, n_x, n_z = count // 2, count // 8, count // 32

    def span(start, size):
        return pl.ds(pl.multiple_of(start, size), size)

    copy = remote(gram.at[span((1 - c) * n_c, n_c), :], half_in, red_send, red_recv, sib)
    copy.start()
    copy.wait_recv()
    half_in[...] += gram[span(c * n_c, n_c), :]
    x_copies = [remote(half_in.at[span(lax.rem(x + d, 4) * n_x, n_x), :], xin.at[d - 1],
                       x_send.at[d - 1], x_recv.at[d - 1], xs[d - 1]) for d in (1, 2, 3)]
    for cp in x_copies:
        cp.start()
    for cp in x_copies:
        cp.wait_recv()
    xin[3] = half_in[span(x * n_x, n_x), :] + xin[0] + xin[1] + xin[2]
    z_copies = [remote(xin.at[3, span(lax.rem(z + d, 4) * n_z, n_z), :], zin.at[d - 1],
                       z_send.at[d - 1], z_recv.at[d - 1], zs[d - 1]) for d in (1, 2, 3)]
    for cp in z_copies:
        cp.start()
    for cp in z_copies:
        cp.wait_recv()
    zin[3] = xin[3, span(z * n_z, n_z), :] + zin[0] + zin[1] + zin[2]
    y_copies = [remote(zin.at[3], yin.at[d - 1], y_send.at[d - 1], y_recv.at[d - 1], ys[d - 1]) for d in (1, 2, 3)]
    for cp in y_copies:
        cp.start()
    for k in range(EARLY, PARTS):
        for cc in range(2):
            s_copy(cc, k).start()
    for k in range(PARTS):
        for cc in range(2):
            q_copy(cc, k).start()
    for cp in y_copies:
        cp.wait_recv()
    at_z = span(c * n_c + x * n_x + z * n_z, n_z)
    at_x = span(c * n_c + x * n_x, n_x)
    at_c = span(c * n_c, n_c)
    full[at_z, :] = zin[3] + yin[0] + yin[1] + yin[2]

    gz_copies = [remote(full.at[at_z, :], full.at[at_z, :], gz_send.at[d - 1], gz_recv.at[d - 1], zs[d - 1])
                 for d in (1, 2, 3)]
    for cp in gz_copies:
        cp.start()
    for cp in gz_copies:
        cp.wait_recv()
    gx_copies = [remote(full.at[at_x, :], full.at[at_x, :], gx_send.at[d - 1], gx_recv.at[d - 1], xs[d - 1])
                 for d in (1, 2, 3)]
    for cp in gx_copies:
        cp.start()
    for cp in gx_copies:
        cp.wait_recv()
    gc_copy = remote(full.at[at_c, :], full.at[at_c, :], gc_send, gc_recv, sib)
    gc_copy.start()
    gc_copy.wait_recv()

    pair = 2 * rows
    one = spread[:, :1]

    def diagonal(size, row0, col0, axis):
        tile = full[span(row0, size), :] if axis == 1 else full[...]
        r = lax.broadcasted_iota(jnp.int32, tile.shape, 0) + row0
        q = lax.broadcasted_iota(jnp.int32, tile.shape, 1)
        return jnp.sum(jnp.where(r == q, tile, 0.0), axis=axis, keepdims=True)

    own_sq = diagonal(pair, h * pair, 0, 1)
    all_sq = diagonal(count, 0, 0, 0)
    kern = jnp.exp(-(own_sq + all_sq - 2.0 * full[span(h * pair, pair), :]) / one)
    w_ref[...] = jnp.broadcast_to(jnp.sum(kern, axis=1, keepdims=True), w_ref.shape)
    low, high = kern[:, :pair], kern[:, pair:]
    first = h == 0
    k_own[...] = jnp.where(first, low, high)
    k_oth[...] = jnp.where(first, high, low)

    step = jnp.full((1, 128), scal[1], jnp.float32)[:, :1]
    gain = step / jnp.float32(count)
    keep = 1.0 + gain * pull * w_ref[:, :1]
    own_rows, oth_rows = span(h * pair, pair), span((1 - h) * pair, pair)

    def out_copies(gi, k):
        where = cols(c, side[gi], k, piece)
        local = pltpu.make_async_copy(ob.at[gi, k, mine(c), :], out_ref.at[:, where], o_local.at[gi, k])
        away = remote(ob.at[gi, k, mine(1 - c), :], out_ref.at[:, where], o_send.at[gi, k], o_recv.at[gi, k], sib)
        return local, away

    for gi in range(2):
        sib_copy(1, gi).wait_recv()
        if gi == 1:
            sib_copy(0, 1).wait_recv()

        def update(k, carry, gi=gi):
            for cc in range(2):
                if gi == 0:
                    arrival(sb, 0, cc, k, s_send, s_recv).wait_recv()
                else:
                    arrival(sb, 1, cc, k, q_send, q_recv).wait_recv()
            particles = pb[gi, own_rows, kcols(k)]
            q_own = sb[gi, own_rows, kcols(k)] - pull * particles
            q_oth = sb[gi, oth_rows, kcols(k)]
            if gi == 0:
                q_oth = q_oth - pull * pb[0, oth_rows, kcols(k)]
            total = jnp.dot(k_own[...], q_own, precision=lax.Precision.HIGHEST, preferred_element_type=jnp.float32)
            total += jnp.dot(k_oth[...], q_oth, precision=lax.Precision.HIGHEST, preferred_element_type=jnp.float32)
            ob[gi, k] = keep * particles + gain * total
            local, away = out_copies(gi, k)
            away.start()
            local.start()
            return carry

        lax.fori_loop(0, PARTS, update, 0)

    for k in range(PARTS):
        for cc in range(2):
            p_copy(cc, k).wait_send()
            s_copy(cc, k).wait_send()
            q_copy(cc, k).wait_send()
    for n in range(2):
        for gi in range(2):
            sib_copy(n, gi).wait_send()
    copy.wait_send()
    for cp in (*x_copies, *z_copies, *y_copies, *gz_copies, *gx_copies, gc_copy):
        cp.wait_send()
    for gi in range(2):
        for k in range(PARTS):
            local, away = out_copies(gi, k)
            local.wait()
            away.wait()


def solution(mesh):
    size_dom = mesh.shape["dom"]

    def on_device(particles, scores, spread, step_size):
        rows, width = particles.shape
        quarter = width // 4
        piece = quarter // PARTS
        count = size_dom * rows
        scal = jnp.stack([spread, step_size])
        dma = pltpu.SemaphoreType.DMA
        f32 = jnp.float32
        return pl.pallas_call(
            functools.partial(body, size_dom, rows, quarter),
            out_shape=jax.ShapeDtypeStruct(particles.shape, f32),
            in_specs=[pl.BlockSpec(memory_space=pltpu.SMEM), pl.BlockSpec(memory_space=pl.ANY),
                      pl.BlockSpec(memory_space=pl.ANY)],
            out_specs=pl.BlockSpec(memory_space=pl.ANY),
            scratch_shapes=[
                pltpu.VMEM((2, count, quarter), f32),
                pltpu.VMEM((2, count, quarter), f32),
                pltpu.VMEM((2, rows, quarter), f32),
                pltpu.VMEM((2, rows, quarter), f32),
                pltpu.VMEM((2, PARTS, 2 * rows, piece), f32),
                pltpu.VMEM((count, count), f32),
                pltpu.VMEM((count // 2, count), f32),
                pltpu.VMEM((4, count // 8, count), f32),
                pltpu.VMEM((4, count // 32, count), f32),
                pltpu.VMEM((3, count // 32, count), f32),
                pltpu.VMEM((count, count), f32),
                pltpu.VMEM((2 * rows, 2 * rows), f32),
                pltpu.VMEM((2 * rows, 2 * rows), f32),
                pltpu.VMEM((2 * rows, 128), f32),
                dma((8,)), dma((2, 2)), dma((2, 2)),
                dma((2, PARTS)), dma((2, PARTS)), dma((2, PARTS)), dma((2, PARTS)), dma((2, PARTS)), dma((2, PARTS)),
                dma, dma, dma((3,)), dma((3,)), dma((3,)), dma((3,)), dma((3,)), dma((3,)),
                dma((3,)), dma((3,)), dma((3,)), dma((3,)), dma, dma,
                dma((2, PARTS)), dma((2, PARTS)), dma((2, PARTS)),
            ],
            compiler_params=pltpu.CompilerParams(
                collective_id=0, has_side_effects=True, vmem_limit_bytes=58 << 20),
            name="svgd",
        )(scal, particles, scores)

    return jax.shard_map(
        on_device,
        mesh=mesh,
        in_specs=(P("dom", "dim"), P("dom", "dim"), P(), P()),
        out_specs=P("dom", "dim"),
        check_vma=False,
    )
```

time: 262 us -> 156 us (0.60)
  waiting for transfers between devices: 157 us -> 0 us
  Pallas kernels: 0 us -> 149 us
  matrix products: 47.1 us -> 0 us
  starting transfers between devices: 30 us -> 0 us
  between operations: 14.8 us -> 1.31 us
  other arithmetic: 9.76 us -> 0.59 us
    pallas_call x0 -> x1, Pallas kernels: none -> 149 us  [on_device(): pl.pallas_call(functools.partial(body, size_dom, rows, quarter), out_shap...]
    all_gather x2 -> x0, waiting for transfers between devices: 141 us -> none  [the longest x1 102 us: on_device(): gathered = lax.all_gather(particles, 'dom', axis=0, tiled=True)]
    dot_general x3 -> x0, matrix products: 47.1 us -> none  [the longest x1 17.7 us: on_device(): lax.dot_general(particles, gathered, (((1,), (1,)), ((), ())), precision=...]
    all_to_all x4 -> x0, starting transfers between devices: 30 us -> none  [the longest x2 15.2 us: from_everyone(): lax.all_to_all(jnp.broadcast_to(array[None], (devices, *array.shape)), ax...]
    all_to_all x4 -> x0, waiting for transfers between devices: 14.8 us -> none  [the longest x2 7.48 us: sum_at_owner(): lax.all_to_all(blocks, axis, split_axis=0, concat_axis=0, tiled=True)]
    reduce_sum x6 -> x0, other arithmetic: 9.68 us -> none  [the longest x1 6.96 us: on_device(): norms = jnp.sum(gathered * gathered, axis=1)]
    unnamed x0 -> x1, local copies, waits for them, and re-layouts: none -> 4.61 us
  transfers between devices with their start and end apart: 6 -> 0, of which waited for: 4 -> 0; matrix products, arithmetic and copies ran while one was open for 17% -> 0% of each run, Pallas kernels for 0% -> 0%
where the time goes in v1:
time: 156 us
  Pallas kernels  149 us (96%)
  local copies, waits for them, and re-layouts  4.61 us (3%)
    pallas_call x1, Pallas kernels, on_device(): pl.pallas_call(functools.partial(body, size_dom, rows, quarter), out_shap...  149 us
    unnamed x1, local copies, waits for them, and re-layouts  4.61 us

profile of v1, /device:TPU:1, one launch (start us, length us, event | category | flops | bytes accessed | tf_op | source)
XLA Modules:
  0.0 155.6 jit_solution(574226077324125043)
XLA Ops:
  1.3 0.6 pad_maximum_fusion.scal
  1.9 149.1 %svgd.1 = f32[128,8192]{1,0:T(8,128)} custom-call(f32[2]{0:T(128)} %pad_maximum_fusion.scal, f32[128,8192]{1,0:T(8,128)} %p_ref.1, f32[128,8192]{1,0:T(8,128)} %s_ref.1), custom_call_target="tpu_custom_call" | custom-call | tf_op jit(solution)/shard_map/svgd/pallas_call | solution.py:271
  151.0 4.6 %copy.8 = f32[128,8192]{1,0:T(8,128)} copy(f32[128,8192]{1,0:T(8,128)} %svgd.1) | data formatting | bytes 8388608

commit v2 on v1

--- a/solution.py
+++ b/solution.py
@@ -10,18 +10,19 @@
 MESH = pl.DeviceIdType.MESH
 PARTS = 4
 EARLY = 3
+LAST = (4, 4, 4, 2, 1, 1)
 
 
 def body(
     size_dom, rows, quarter,
-    scal, p_ref, s_ref, out_ref,
+    spread_ref, step_ref, p_ref, s_ref, out_ref,
     pb, sb, pt, qs, ob, gram, half_in, xin, zin, yin, full, k_own, k_oth, w_ref,
     load_sem, sib_send, sib_recv, p_send, p_recv, s_send, s_recv, q_send, q_recv,
     red_send, red_recv, x_send, x_recv, z_send, z_recv, y_send, y_recv,
     gz_send, gz_recv, gx_send, gx_recv, gc_send, gc_recv,
-    o_local, o_send, o_recv,
+    o_send, o_recv,
 ):
-    piece = quarter // PARTS
+    piece, unit = quarter // PARTS, quarter // 16
     dom, dim = lax.axis_index("dom"), lax.axis_index("dim")
     h, c = dom // 2, lax.rem(dom, 2)
     z, lo, x = dim // 8, lax.rem(dim // 4, 2), lax.rem(dim, 4)
@@ -72,12 +73,14 @@
         return remote(s_ref.at[:, cols(cc, 1 - h, k, piece)], sb.at[0, mine(block), kcols(k)],
                       s_send.at[cc, k], s_recv.at[c, k], over[cc])
 
-    def q_copy(cc, k):
-        return remote(qs.at[cc, :, kcols(k)], sb.at[1, mine(block), kcols(k)],
-                      q_send.at[cc, k], q_recv.at[c, k], over[cc])
-
-    def arrival(buf, gi, cc, k, ssem, rsem):
-        there = buf.at[gi, mine((1 - h) * 2 + cc), kcols(k)]
+    last_at = [pl.ds(unit * sum(LAST[:n]), unit * width) for n, width in enumerate(LAST)]
+
+    def q_copy(cc, n):
+        return remote(qs.at[cc, :, last_at[n]], sb.at[1, mine(block), last_at[n]],
+                      q_send.at[cc, n], q_recv.at[c, n], over[cc])
+
+    def arrival(buf, gi, cc, k, at, ssem, rsem):
+        there = buf.at[gi, mine((1 - h) * 2 + cc), at]
         return remote(there, there, ssem.at[cc, k], rsem.at[cc, k], over[cc])
 
     def sib_copy(n, gi):
@@ -107,7 +110,7 @@
     for load in loads:
         load.wait()
 
-    spread = jnp.full((1, 128), scal[0], jnp.float32)
+    spread = jnp.full((1, 128), spread_ref[0], jnp.float32)
     pull = (2.0 / spread)[:, :1]
     for cc in range(2):
         def scale(k, carry, cc=cc):
@@ -120,7 +123,7 @@
 
     def gram_step(k, carry):
         for cc in range(2):
-            arrival(pb, 0, cc, k, p_send, p_recv).wait_recv()
+            arrival(pb, 0, cc, k, kcols(k), p_send, p_recv).wait_recv()
         part = pb[0, :, kcols(k)]
         gram[...] += lax.dot_general(part, part, (((1,), (1,)), ((), ())),
                                      precision=lax.Precision.HIGHEST, preferred_element_type=jnp.float32)
@@ -158,9 +161,9 @@
     for k in range(EARLY, PARTS):
         for cc in range(2):
             s_copy(cc, k).start()
-    for k in range(PARTS):
-        for cc in range(2):
-            q_copy(cc, k).start()
+    for n in range(len(LAST)):
+        for cc in range(2):
+            q_copy(cc, n).start()
     for cp in y_copies:
         cp.wait_recv()
     at_z = span(c * n_c + x * n_x + z * n_z, n_z)
@@ -196,65 +199,77 @@
     own_sq = diagonal(pair, h * pair, 0, 1)
     all_sq = diagonal(count, 0, 0, 0)
     kern = jnp.exp(-(own_sq + all_sq - 2.0 * full[span(h * pair, pair), :]) / one)
-    w_ref[...] = jnp.broadcast_to(jnp.sum(kern, axis=1, keepdims=True), w_ref.shape)
+    step = jnp.full((1, 128), step_ref[0], jnp.float32)[:, :1]
+    gain = step / jnp.float32(count)
+    w_ref[...] = jnp.broadcast_to(1.0 + gain * pull * jnp.sum(kern, axis=1, keepdims=True), w_ref.shape)
+    kern = gain * kern
     low, high = kern[:, :pair], kern[:, pair:]
     first = h == 0
     k_own[...] = jnp.where(first, low, high)
     k_oth[...] = jnp.where(first, high, low)
-
-    step = jnp.full((1, 128), scal[1], jnp.float32)[:, :1]
-    gain = step / jnp.float32(count)
-    keep = 1.0 + gain * pull * w_ref[:, :1]
     own_rows, oth_rows = span(h * pair, pair), span((1 - h) * pair, pair)
 
-    def out_copies(gi, k):
-        where = cols(c, side[gi], k, piece)
-        local = pltpu.make_async_copy(ob.at[gi, k, mine(c), :], out_ref.at[:, where], o_local.at[gi, k])
-        away = remote(ob.at[gi, k, mine(1 - c), :], out_ref.at[:, where], o_send.at[gi, k], o_recv.at[gi, k], sib)
-        return local, away
-
-    for gi in range(2):
-        sib_copy(1, gi).wait_recv()
-        if gi == 1:
-            sib_copy(0, 1).wait_recv()
-
-        def update(k, carry, gi=gi):
-            for cc in range(2):
-                if gi == 0:
-                    arrival(sb, 0, cc, k, s_send, s_recv).wait_recv()
-                else:
-                    arrival(sb, 1, cc, k, q_send, q_recv).wait_recv()
-            particles = pb[gi, own_rows, kcols(k)]
-            q_own = sb[gi, own_rows, kcols(k)] - pull * particles
-            q_oth = sb[gi, oth_rows, kcols(k)]
-            if gi == 0:
-                q_oth = q_oth - pull * pb[0, oth_rows, kcols(k)]
-            total = jnp.dot(k_own[...], q_own, precision=lax.Precision.HIGHEST, preferred_element_type=jnp.float32)
-            total += jnp.dot(k_oth[...], q_oth, precision=lax.Precision.HIGHEST, preferred_element_type=jnp.float32)
-            ob[gi, k] = keep * particles + gain * total
-            local, away = out_copies(gi, k)
-            away.start()
-            local.start()
-            return carry
-
-        lax.fori_loop(0, PARTS, update, 0)
+    def product(k_ref, value):
+        return jnp.dot(k_ref[...], value, precision=lax.Precision.HIGHEST, preferred_element_type=jnp.float32)
+
+    def of_chip(gi, k):
+        particles = pb[gi, own_rows, kcols(k)]
+        return w_ref[:, :1] * particles + product(k_own, sb[gi, own_rows, kcols(k)] - pull * particles)
+
+    def first_out(k):
+        return remote(ob.at[0, mine(1 - c), kcols(k)], out_ref.at[:, cols(c, h, k, piece)],
+                      o_send.at[k], o_recv.at[k], sib)
+
+    def last_out(n):
+        where = pl.ds(pl.multiple_of(c * (2 * quarter) + (1 - h) * quarter + unit * sum(LAST[:n]), unit), unit * LAST[n])
+        return where, remote(ob.at[1, mine(1 - c), last_at[n]], out_ref.at[:, where],
+                             o_send.at[PARTS + n], o_recv.at[PARTS + n], sib)
+
+    sib_copy(1, 0).wait_recv()
+
+    def first_step(k, carry):
+        for cc in range(2):
+            arrival(sb, 0, cc, k, kcols(k), s_send, s_recv).wait_recv()
+        q_oth = sb[0, oth_rows, kcols(k)] - pull * pb[0, oth_rows, kcols(k)]
+        ob[0, :, kcols(k)] = of_chip(0, k) + product(k_oth, q_oth)
+        first_out(k).start()
+        out_ref[:, cols(c, h, k, piece)] = ob[0, mine(c), kcols(k)]
+        return carry
+
+    lax.fori_loop(0, PARTS, first_step, 0)
+    sib_copy(0, 1).wait_recv()
+    sib_copy(1, 1).wait_recv()
+
+    def base_step(k, carry):
+        ob[1, :, kcols(k)] = of_chip(1, k)
+        return carry
+
+    lax.fori_loop(0, PARTS, base_step, 0)
+    for n in range(len(LAST)):
+        for cc in range(2):
+            arrival(sb, 1, cc, n, last_at[n], q_send, q_recv).wait_recv()
+        ob[1, :, last_at[n]] = ob[1, :, last_at[n]] + product(k_oth, sb[1, oth_rows, last_at[n]])
+        where, away = last_out(n)
+        away.start()
+        out_ref[:, where] = ob[1, mine(c), last_at[n]]
 
     for k in range(PARTS):
         for cc in range(2):
             p_copy(cc, k).wait_send()
             s_copy(cc, k).wait_send()
-            q_copy(cc, k).wait_send()
+    for n in range(len(LAST)):
+        for cc in range(2):
+            q_copy(cc, n).wait_send()
     for n in range(2):
         for gi in range(2):
             sib_copy(n, gi).wait_send()
     copy.wait_send()
     for cp in (*x_copies, *z_copies, *y_copies, *gz_copies, *gx_copies, gc_copy):
         cp.wait_send()
-    for gi in range(2):
-        for k in range(PARTS):
-            local, away = out_copies(gi, k)
-            local.wait()
-            away.wait()
+    for k in range(PARTS):
+        first_out(k).wait()
+    for n in range(len(LAST)):
+        last_out(n)[1].wait()
 
 
 def solution(mesh):
@@ -265,21 +280,20 @@
         quarter = width // 4
         piece = quarter // PARTS
         count = size_dom * rows
-        scal = jnp.stack([spread, step_size])
         dma = pltpu.SemaphoreType.DMA
         f32 = jnp.float32
         return pl.pallas_call(
             functools.partial(body, size_dom, rows, quarter),
             out_shape=jax.ShapeDtypeStruct(particles.shape, f32),
-            in_specs=[pl.BlockSpec(memory_space=pltpu.SMEM), pl.BlockSpec(memory_space=pl.ANY),
-                      pl.BlockSpec(memory_space=pl.ANY)],
-            out_specs=pl.BlockSpec(memory_space=pl.ANY),
+            in_specs=[pl.BlockSpec(memory_space=pltpu.SMEM), pl.BlockSpec(memory_space=pltpu.SMEM), pl.BlockSpec(memory_space=pltpu.HBM),
+                      pl.BlockSpec(memory_space=pltpu.HBM)],
+            out_specs=pl.BlockSpec(memory_space=pltpu.VMEM),
             scratch_shapes=[
                 pltpu.VMEM((2, count, quarter), f32),
                 pltpu.VMEM((2, count, quarter), f32),
                 pltpu.VMEM((2, rows, quarter), f32),
                 pltpu.VMEM((2, rows, quarter), f32),
-                pltpu.VMEM((2, PARTS, 2 * rows, piece), f32),
+                pltpu.VMEM((2, 2 * rows, quarter), f32),
                 pltpu.VMEM((count, count), f32),
                 pltpu.VMEM((count // 2, count), f32),
                 pltpu.VMEM((4, count // 8, count), f32),
@@ -290,15 +304,16 @@
                 pltpu.VMEM((2 * rows, 2 * rows), f32),
                 pltpu.VMEM((2 * rows, 128), f32),
                 dma((8,)), dma((2, 2)), dma((2, 2)),
-                dma((2, PARTS)), dma((2, PARTS)), dma((2, PARTS)), dma((2, PARTS)), dma((2, PARTS)), dma((2, PARTS)),
+                dma((2, PARTS)), dma((2, PARTS)), dma((2, PARTS)), dma((2, PARTS)),
+                dma((2, len(LAST))), dma((2, len(LAST))),
                 dma, dma, dma((3,)), dma((3,)), dma((3,)), dma((3,)), dma((3,)), dma((3,)),
                 dma((3,)), dma((3,)), dma((3,)), dma((3,)), dma, dma,
-                dma((2, PARTS)), dma((2, PARTS)), dma((2, PARTS)),
+                dma((PARTS + len(LAST),)), dma((PARTS + len(LAST),)),
             ],
             compiler_params=pltpu.CompilerParams(
-                collective_id=0, has_side_effects=True, vmem_limit_bytes=58 << 20),
+                collective_id=0, has_side_effects=True, vmem_limit_bytes=48 << 20),
             name="svgd",
-        )(scal, particles, scores)
+        )(spread.reshape(1), step_size.reshape(1), particles, scores)
 
     return jax.shard_map(
         on_device,

time: 156 us -> 151 us (0.968)
  local copies, waits for them, and re-layouts: 4.61 us -> 2.02 us
    unnamed x1, local copies, waits for them, and re-layouts: 4.61 us -> 2.02 us
    pallas_call x1, Pallas kernels: 149 us -> 148 us  [on_device(): pl.pallas_call(functools.partial(body, size_dom, rows, quarter), out_shap...]
where the time goes in v2:
time: 151 us
  Pallas kernels  148 us (98%)
  local copies, waits for them, and re-layouts  2.02 us (1%)
    pallas_call x1, Pallas kernels, on_device(): pl.pallas_call(functools.partial(body, size_dom, rows, quarter), out_shap...  148 us

profile of v2, /device:TPU:1, one launch (start us, length us, event | category | flops | bytes accessed | tf_op | source)
XLA Modules:
  0.0 150.8 jit_solution(11797744844448432238)
XLA Ops:
  1.3 147.5 %svgd.1 = f32[128,8192]{1,0:T(8,128)S(1)} custom-call(f32[1]{0:T(128)} %bitcast.2.spread_ref, f32[1]{0:T(128)} %bitcast.3.step_ref, f32[128,8192]{1,0:T(8,128)} %p_ref.1, f32[128,8192]{1,0:T(8,128)} %s_ref.1), custom_call_target="tpu_custom_call" | custom-call | tf_op jit(solution)/shard_map/svgd/pallas_call | solution.py:285
  148.8 2.0 %copy.8 = f32[128,8192]{1,0:T(8,128)} copy(f32[128,8192]{1,0:T(8,128)S(1)} %svgd.1) | data formatting | bytes 8388608

commit v3 on v2

--- a/solution.py
+++ b/solution.py
@@ -20,7 +20,7 @@
     load_sem, sib_send, sib_recv, p_send, p_recv, s_send, s_recv, q_send, q_recv,
     red_send, red_recv, x_send, x_recv, z_send, z_recv, y_send, y_recv,
     gz_send, gz_recv, gx_send, gx_recv, gc_send, gc_recv,
-    o_send, o_recv,
+    o_send, o_recv, met,
 ):
     piece, unit = quarter // PARTS, quarter // 16
     dom, dim = lax.axis_index("dom"), lax.axis_index("dim")
@@ -40,13 +40,22 @@
     for d in (1, 2, 3):
         yy = lax.rem(y + d, 4)
         ys.append(dev(yy // 2, c, z, lax.rem(yy, 2), x))
-    cross = dev(1 - h, 1 - c, z, lo, x)
 
     barrier = pltpu.get_barrier_semaphore()
-    peers = [sib, cross, *xs, *zs, *ys]
-    for peer in peers:
+    near = [sib, *over]
+    wide = [*xs, *zs, ys[0], ys[2]]
+    for peer in near:
         pl.semaphore_signal(barrier, inc=1, device_id=peer, device_id_type=MESH)
-    pl.semaphore_wait(barrier, len(peers))
+
+    @pl.when(c == 0)
+    def _():
+        for peer in wide:
+            pl.semaphore_signal(barrier, inc=1, device_id=peer, device_id_type=MESH)
+        pl.semaphore_wait(barrier, len(near) + len(wide))
+
+    @pl.when(c == 1)
+    def _():
+        pl.semaphore_wait(barrier, len(near))
 
     def remote(src, dst, ssem, rsem, to):
         return pltpu.make_async_remote_copy(
@@ -91,6 +100,11 @@
     for k in range(PARTS):
         for cc in range(2):
             p_copy(cc, k).start()
+    @pl.when(c == 0)
+    def _():
+        for peer in wide:
+            pl.semaphore_signal(met, inc=1, device_id=peer, device_id_type=MESH)
+
     loads = []
     for n, (src, dst) in enumerate(((p_ref, pb), (s_ref, sb))):
         for gi in range(2):
@@ -136,6 +150,15 @@
 
     def span(start, size):
         return pl.ds(pl.multiple_of(start, size), size)
+
+    @pl.when(c == 0)
+    def _():
+        pl.semaphore_wait(met, len(wide))
+        pl.semaphore_signal(met, inc=1, device_id=sib, device_id_type=MESH)
+
+    @pl.when(c == 1)
+    def _():
+        pl.semaphore_wait(met, 1)
 
     copy = remote(gram.at[span((1 - c) * n_c, n_c), :], half_in, red_send, red_recv, sib)
     copy.start()
@@ -309,6 +332,7 @@
                 dma, dma, dma((3,)), dma((3,)), dma((3,)), dma((3,)), dma((3,)), dma((3,)),
                 dma((3,)), dma((3,)), dma((3,)), dma((3,)), dma, dma,
                 dma((PARTS + len(LAST),)), dma((PARTS + len(LAST),)),
+                pltpu.SemaphoreType.REGULAR,
             ],
             compiler_params=pltpu.CompilerParams(
                 collective_id=0, has_side_effects=True, vmem_limit_bytes=48 << 20),

time: 151 us -> 148 us (0.980)
  Pallas kernels: 148 us -> 144 us
    pallas_call x1, Pallas kernels: 148 us -> 144 us  [on_device(): pl.pallas_call(functools.partial(body, size_dom, rows, quarter), out_shap...]
where the time goes in v3:
time: 148 us
  Pallas kernels  144 us (97%)
  local copies, waits for them, and re-layouts  2.02 us (1%)
    pallas_call x1, Pallas kernels, on_device(): pl.pallas_call(functools.partial(body, size_dom, rows, quarter), out_shap...  144 us

profile of v3, /device:TPU:1, one launch (start us, length us, event | category | flops | bytes accessed | tf_op | source)
XLA Modules:
  0.0 147.7 jit_solution(3683701659694608575)
XLA Ops:
  1.3 144.4 %svgd.1 = f32[128,8192]{1,0:T(8,128)S(1)} custom-call(f32[1]{0:T(128)} %bitcast.2.spread_ref, f32[1]{0:T(128)} %bitcast.3.step_ref, f32[128,8192]{1,0:T(8,128)} %p_ref.1, f32[128,8192]{1,0:T(8,128)} %s_ref.1), custom_call_target="tpu_custom_call" | custom-call | tf_op jit(solution)/shard_map/svgd/pallas_call | solution.py:308
  145.7 2.0 %copy.8 = f32[128,8192]{1,0:T(8,128)} copy(f32[128,8192]{1,0:T(8,128)S(1)} %svgd.1) | data formatting | bytes 8388608

commit v4 on v3

--- a/solution.py
+++ b/solution.py
@@ -16,7 +16,7 @@
 def body(
     size_dom, rows, quarter,
     spread_ref, step_ref, p_ref, s_ref, out_ref,
-    pb, sb, pt, qs, ob, gram, half_in, xin, zin, yin, full, k_own, k_oth, w_ref,
+    pb, sb, pt, qs, first, ob, gram, half_in, xin, zin, yin, full, k_own, k_oth, w_ref,
     load_sem, sib_send, sib_recv, p_send, p_recv, s_send, s_recv, q_send, q_recv,
     red_send, red_recv, x_send, x_recv, z_send, z_recv, y_send, y_recv,
     gz_send, gz_recv, gx_send, gx_recv, gc_send, gc_recv,
@@ -41,6 +41,11 @@
         yy = lax.rem(y + d, 4)
         ys.append(dev(yy // 2, c, z, lax.rem(yy, 2), x))
 
+    ahead = [pltpu.make_async_copy(p_ref.at[:, pl.ds(pl.multiple_of(cc * (2 * quarter) + (1 - h) * quarter, piece), piece)],
+                                   first.at[cc], load_sem.at[8 + cc]) for cc in range(2)]
+    for load in ahead:
+        load.start()
+
     barrier = pltpu.get_barrier_semaphore()
     near = [sib, *over]
     wide = [*xs, *zs, ys[0], ys[2]]
@@ -75,7 +80,8 @@
     side = [h, 1 - h]
 
     def p_copy(cc, k):
-        return remote(p_ref.at[:, cols(cc, 1 - h, k, piece)], pb.at[0, mine(block), kcols(k)],
+        source = first.at[cc] if k == 0 else p_ref.at[:, cols(cc, 1 - h, k, piece)]
+        return remote(source, pb.at[0, mine(block), kcols(k)],
                       p_send.at[cc, k], p_recv.at[c, k], over[cc])
 
     def s_copy(cc, k):
@@ -99,6 +105,8 @@
 
     for k in range(PARTS):
         for cc in range(2):
+            if k == 0:
+                ahead[cc].wait()
             p_copy(cc, k).start()
     @pl.when(c == 0)
     def _():
@@ -178,21 +186,49 @@
     for cp in z_copies:
         cp.wait_recv()
     zin[3] = xin[3, span(z * n_z, n_z), :] + zin[0] + zin[1] + zin[2]
-    y_copies = [remote(zin.at[3], yin.at[d - 1], y_send.at[d - 1], y_recv.at[d - 1], ys[d - 1]) for d in (1, 2, 3)]
-    for cp in y_copies:
-        cp.start()
+    tile = pl.ds(pl.multiple_of((c * 2 + x // 2) * 128, 128), 128)
+
+    def y_copy(d, whole):
+        src, dst = zin.at[3], yin.at[d - 1]
+        if not whole:
+            src, dst = src.at[:, tile], dst.at[:, tile]
+        return remote(src, dst, y_send.at[d - 1], y_recv.at[d - 1], ys[d - 1])
+
+    def on_y(act, of):
+        for d in (1, 2, 3):
+            use = of(d)
+
+            @pl.when(use == c)
+            def _(d=d):
+                act(y_copy(d, True))
+
+            @pl.when(use != c)
+            def _(d=d):
+                act(y_copy(d, False))
+
+    def receiver(d):
+        return lax.rem(y + d, 4) // 2
+
+    on_y(lambda cp: cp.start(), receiver)
     for k in range(EARLY, PARTS):
         for cc in range(2):
             s_copy(cc, k).start()
     for n in range(len(LAST)):
         for cc in range(2):
             q_copy(cc, n).start()
-    for cp in y_copies:
-        cp.wait_recv()
+    on_y(lambda cp: cp.wait_recv(), lambda d: h)
     at_z = span(c * n_c + x * n_x + z * n_z, n_z)
     at_x = span(c * n_c + x * n_x, n_x)
     at_c = span(c * n_c, n_c)
-    full[at_z, :] = zin[3] + yin[0] + yin[1] + yin[2]
+
+    @pl.when(h == c)
+    def _():
+        full[at_z, :] = zin[3] + yin[0] + yin[1] + yin[2]
+
+    @pl.when(h != c)
+    def _():
+        full[at_z, :] = zin[3]
+        full[at_z, tile] = zin[3, :, tile] + yin[0, :, tile] + yin[1, :, tile] + yin[2, :, tile]
 
     gz_copies = [remote(full.at[at_z, :], full.at[at_z, :], gz_send.at[d - 1], gz_recv.at[d - 1], zs[d - 1])
                  for d in (1, 2, 3)]
@@ -227,9 +263,9 @@
     w_ref[...] = jnp.broadcast_to(1.0 + gain * pull * jnp.sum(kern, axis=1, keepdims=True), w_ref.shape)
     kern = gain * kern
     low, high = kern[:, :pair], kern[:, pair:]
-    first = h == 0
-    k_own[...] = jnp.where(first, low, high)
-    k_oth[...] = jnp.where(first, high, low)
+    upper = h == 0
+    k_own[...] = jnp.where(upper, low, high)
+    k_oth[...] = jnp.where(upper, high, low)
     own_rows, oth_rows = span(h * pair, pair), span((1 - h) * pair, pair)
 
     def product(k_ref, value):
@@ -271,10 +307,11 @@
     for n in range(len(LAST)):
         for cc in range(2):
             arrival(sb, 1, cc, n, last_at[n], q_send, q_recv).wait_recv()
-        ob[1, :, last_at[n]] = ob[1, :, last_at[n]] + product(k_oth, sb[1, oth_rows, last_at[n]])
+        q_oth = sb[1, oth_rows, last_at[n]]
         where, away = last_out(n)
+        ob[1, mine(1 - c), last_at[n]] = ob[1, mine(1 - c), last_at[n]] + product(k_oth.at[mine(1 - c), :], q_oth)
         away.start()
-        out_ref[:, where] = ob[1, mine(c), last_at[n]]
+        out_ref[:, where] = ob[1, mine(c), last_at[n]] + product(k_oth.at[mine(c), :], q_oth)
 
     for k in range(PARTS):
         for cc in range(2):
@@ -287,7 +324,8 @@
         for gi in range(2):
             sib_copy(n, gi).wait_send()
     copy.wait_send()
-    for cp in (*x_copies, *z_copies, *y_copies, *gz_copies, *gx_copies, gc_copy):
+    on_y(lambda cp: cp.wait_send(), receiver)
+    for cp in (*x_copies, *z_copies, *gz_copies, *gx_copies, gc_copy):
         cp.wait_send()
     for k in range(PARTS):
         first_out(k).wait()
@@ -316,6 +354,7 @@
                 pltpu.VMEM((2, count, quarter), f32),
                 pltpu.VMEM((2, rows, quarter), f32),
                 pltpu.VMEM((2, rows, quarter), f32),
+                pltpu.VMEM((2, rows, piece), f32),
                 pltpu.VMEM((2, 2 * rows, quarter), f32),
                 pltpu.VMEM((count, count), f32),
                 pltpu.VMEM((count // 2, count), f32),
@@ -326,7 +365,7 @@
                 pltpu.VMEM((2 * rows, 2 * rows), f32),
                 pltpu.VMEM((2 * rows, 2 * rows), f32),
                 pltpu.VMEM((2 * rows, 128), f32),
-                dma((8,)), dma((2, 2)), dma((2, 2)),
+                dma((10,)), dma((2, 2)), dma((2, 2)),
                 dma((2, PARTS)), dma((2, PARTS)), dma((2, PARTS)), dma((2, PARTS)),
                 dma((2, len(LAST))), dma((2, len(LAST))),
                 dma, dma, dma((3,)), dma((3,)), dma((3,)), dma((3,)), dma((3,)), dma((3,)),

time: 148 us -> 147 us (level)
  no operation moved by 1% of the time
where the time goes in v4:
time: 147 us
  Pallas kernels  144 us (98%)
  local copies, waits for them, and re-layouts  2.02 us (1%)
    pallas_call x1, Pallas kernels, on_device(): pl.pallas_call(functools.partial(body, size_dom, rows, quarter), out_shap...  144 us

profile of v4, /device:TPU:1, one launch (start us, length us, event | category | flops | bytes accessed | tf_op | source)
XLA Modules:
  0.0 147.2 jit_solution(3835723181667606515)
XLA Ops:
  1.3 143.8 %svgd.1 = f32[128,8192]{1,0:T(8,128)S(1)} custom-call(f32[1]{0:T(128)} %bitcast.2.spread_ref, f32[1]{0:T(128)} %bitcast.3.step_ref, f32[128,8192]{1,0:T(8,128)} %p_ref.1, f32[128,8192]{1,0:T(8,128)} %s_ref.1), custom_call_target="tpu_custom_call" | custom-call | tf_op jit(solution)/shard_map/svgd/pallas_call | solution.py:346
  145.1 2.0 %copy.8 = f32[128,8192]{1,0:T(8,128)} copy(f32[128,8192]{1,0:T(8,128)S(1)} %svgd.1) | data formatting | bytes 8388608

commit v5 on v4

--- a/solution.py
+++ b/solution.py
@@ -8,9 +8,9 @@
 from jax.sharding import PartitionSpec as P
 
 MESH = pl.DeviceIdType.MESH
-PARTS = 4
-EARLY = 3
-LAST = (4, 4, 4, 2, 1, 1)
+PARTS = 2
+EARLY = 2
+LAST = (8, 4, 2, 1, 1)
 
 
 def body(
@@ -304,22 +304,11 @@
         return carry
 
     lax.fori_loop(0, PARTS, base_step, 0)
-    for n in range(len(LAST)):
-        for cc in range(2):
-            arrival(sb, 1, cc, n, last_at[n], q_send, q_recv).wait_recv()
-        q_oth = sb[1, oth_rows, last_at[n]]
-        where, away = last_out(n)
-        ob[1, mine(1 - c), last_at[n]] = ob[1, mine(1 - c), last_at[n]] + product(k_oth.at[mine(1 - c), :], q_oth)
-        away.start()
-        out_ref[:, where] = ob[1, mine(c), last_at[n]] + product(k_oth.at[mine(c), :], q_oth)
 
     for k in range(PARTS):
         for cc in range(2):
             p_copy(cc, k).wait_send()
             s_copy(cc, k).wait_send()
-    for n in range(len(LAST)):
-        for cc in range(2):
-            q_copy(cc, n).wait_send()
     for n in range(2):
         for gi in range(2):
             sib_copy(n, gi).wait_send()
@@ -329,6 +318,20 @@
         cp.wait_send()
     for k in range(PARTS):
         first_out(k).wait()
+
+    for n in range(len(LAST)):
+        for cc in range(2):
+            if n:
+                q_copy(cc, n - 1).wait_send()
+            arrival(sb, 1, cc, n, last_at[n], q_send, q_recv).wait_recv()
+        q_oth = sb[1, oth_rows, last_at[n]]
+        where, away = last_out(n)
+        ob[1, mine(1 - c), last_at[n]] = ob[1, mine(1 - c), last_at[n]] + product(k_oth.at[mine(1 - c), :], q_oth)
+        away.start()
+        out_ref[:, where] = ob[1, mine(c), last_at[n]] + product(k_oth.at[mine(c), :], q_oth)
+
+    for cc in range(2):
+        q_copy(cc, len(LAST) - 1).wait_send()
     for n in range(len(LAST)):
         last_out(n)[1].wait()
 

time: 147 us -> 147 us (level)
  no operation moved by 1% of the time
where the time goes in v5:
time: 147 us
  Pallas kernels  144 us (98%)
  local copies, waits for them, and re-layouts  2.02 us (1%)
    pallas_call x1, Pallas kernels, on_device(): pl.pallas_call(functools.partial(body, size_dom, rows, quarter), out_shap...  144 us

profile of v5, /device:TPU:1, one launch (start us, length us, event | category | flops | bytes accessed | tf_op | source)
XLA Modules:
  0.0 147.0 jit_solution(13492998727735877996)
XLA Ops:
  1.3 143.7 %svgd.1 = f32[128,8192]{1,0:T(8,128)S(1)} custom-call(f32[1]{0:T(128)} %bitcast.2.spread_ref, f32[1]{0:T(128)} %bitcast.3.step_ref, f32[128,8192]{1,0:T(8,128)} %p_ref.1, f32[128,8192]{1,0:T(8,128)} %s_ref.1), custom_call_target="tpu_custom_call" | custom-call | tf_op jit(solution)/shard_map/svgd/pallas_call | solution.py:349
  145.0 2.0 %copy.8 = f32[128,8192]{1,0:T(8,128)} copy(f32[128,8192]{1,0:T(8,128)S(1)} %svgd.1) | data formatting | bytes 8388608

commit v6 on v4

--- a/solution.py
+++ b/solution.py
@@ -8,9 +8,9 @@
 from jax.sharding import PartitionSpec as P
 
 MESH = pl.DeviceIdType.MESH
-PARTS = 4
-EARLY = 3
-LAST = (4, 4, 4, 2, 1, 1)
+PARTS = 2
+EARLY = 2
+LAST = (8, 4, 2, 1, 1)
 
 
 def body(

time: 147 us -> 147 us (level)
  no operation moved by 1% of the time
where the time goes in v6:
time: 147 us
  Pallas kernels  144 us (98%)
  local copies, waits for them, and re-layouts  2.02 us (1%)
    pallas_call x1, Pallas kernels, on_device(): pl.pallas_call(functools.partial(body, size_dom, rows, quarter), out_shap...  144 us

profile of v6, /device:TPU:1, one launch (start us, length us, event | category | flops | bytes accessed | tf_op | source)
XLA Modules:
  0.0 147.0 jit_solution(424317118450351282)
XLA Ops:
  1.3 143.7 %svgd.1 = f32[128,8192]{1,0:T(8,128)S(1)} custom-call(f32[1]{0:T(128)} %bitcast.2.spread_ref, f32[1]{0:T(128)} %bitcast.3.step_ref, f32[128,8192]{1,0:T(8,128)} %p_ref.1, f32[128,8192]{1,0:T(8,128)} %s_ref.1), custom_call_target="tpu_custom_call" | custom-call | tf_op jit(solution)/shard_map/svgd/pallas_call | solution.py:346
  145.0 2.0 %copy.8 = f32[128,8192]{1,0:T(8,128)} copy(f32[128,8192]{1,0:T(8,128)S(1)} %svgd.1) | data formatting | bytes 8388608

commit v7 on v6

--- a/solution.py
+++ b/solution.py
@@ -132,7 +132,7 @@
     for load in loads:
         load.wait()
 
-    spread = jnp.full((1, 128), spread_ref[0], jnp.float32)
+    spread = jnp.full((1, 128), spread_ref[()], jnp.float32)
     pull = (2.0 / spread)[:, :1]
     for cc in range(2):
         def scale(k, carry, cc=cc):
@@ -258,7 +258,7 @@
     own_sq = diagonal(pair, h * pair, 0, 1)
     all_sq = diagonal(count, 0, 0, 0)
     kern = jnp.exp(-(own_sq + all_sq - 2.0 * full[span(h * pair, pair), :]) / one)
-    step = jnp.full((1, 128), step_ref[0], jnp.float32)[:, :1]
+    step = jnp.full((1, 128), step_ref[()], jnp.float32)[:, :1]
     gain = step / jnp.float32(count)
     w_ref[...] = jnp.broadcast_to(1.0 + gain * pull * jnp.sum(kern, axis=1, keepdims=True), w_ref.shape)
     kern = gain * kern
@@ -376,7 +376,7 @@
             compiler_params=pltpu.CompilerParams(
                 collective_id=0, has_side_effects=True, vmem_limit_bytes=48 << 20),
             name="svgd",
-        )(spread.reshape(1), step_size.reshape(1), particles, scores)
+        )(spread, step_size, particles, scores)
 
     return jax.shard_map(
         on_device,

time: 147 us -> 147 us (level)
  no operation moved by 1% of the time
where the time goes in v7:
time: 147 us
  Pallas kernels  144 us (98%)
  local copies, waits for them, and re-layouts  2.02 us (1%)
    pallas_call x1, Pallas kernels, on_device(): pl.pallas_call(functools.partial(body, size_dom, rows, quarter), out_shap...  144 us

profile of v7, /device:TPU:1, one launch (start us, length us, event | category | flops | bytes accessed | tf_op | source)
XLA Modules:
  0.0 147.0 jit_solution(424317118450351282)
XLA Ops:
  1.3 143.7 %svgd.1 = f32[128,8192]{1,0:T(8,128)S(1)} custom-call(f32[]{:T(128)S(6)} %copy.6.spread_ref, f32[]{:T(128)S(6)} %copy.7.step_ref, f32[128,8192]{1,0:T(8,128)} %p_ref.1, f32[128,8192]{1,0:T(8,128)} %s_ref.1), custom_call_target="tpu_custom_call" | custom-call | tf_op jit(solution)/shard_map/svgd/pallas_call | solution.py:346
  145.0 2.0 %copy.8 = f32[128,8192]{1,0:T(8,128)} copy(f32[128,8192]{1,0:T(8,128)S(1)} %svgd.1) | data formatting | bytes 8388608
